TPU v7x, 32 devices: a whole 2x2x4 slice. The times are simulated.
32 devices in a mesh: dp: 4 (over x, core), fsdp: 8 (over z, y).
Axes of the slice: x: 2, y: 2, z: 4, core: 2. Of those that a mesh axis runs over, the one named last changes fastest.
Arguments:
- hidden: bfloat16 [32, 256, 4096], P(('dp', 'fsdp')), may hold values from -40 to 40
- lengths: int32 [32], P(('dp', 'fsdp')), may hold values from 64 to 256
- list_ids: int32 [32], P('dp'), may hold values from 0 to 255, as said below
- list_owner: int32 [256], replicated, may hold values from 0 to 3, as said below
- attn_gain: float32 [4096], replicated, may hold values from 0.25 to 1.75
- final_gain: float32 [4096], replicated, may hold values from 0.25 to 1.75
- w_query: bfloat16 [4096, 2048], P('fsdp'), may hold values from -24 to 24
- w_key: bfloat16 [4096, 512], P('fsdp'), may hold values from -1 to 1
- w_value: bfloat16 [4096, 512], P('fsdp'), may hold values from -0.09375 to 0.09375
- w_out: bfloat16 [2048, 4096], P('fsdp'), may hold values from -0.125 to 0.125
Outputs:
- inbox: bfloat16 [4, 4, 4, 4096], P('dp', None, None, 'fsdp')
Inputs may be any that keep to these rules, and one draw needn't show every extreme that they name: Positions from lengths[p] on are padding. `list_ids`: in each aligned block of 8 passages (those of one index of dp), at most 4 passages name lists of one owner, and in every block some owner is named by exactly 4 passages. `list_owner`: every owner holds exactly 64 lists.
All inputs are finite; a program needn't handle non-finite values.
Results may differ from a plain program's by a relative error of at most 0.0029.
The roundings to bfloat16 on the way count: a program that leaves them out, or rounds other values in their place, can miss the bound.
Values may be sent and summed in bfloat16 or wider, within the bound.
A program may use at most 64 MiB of HBM per device.

v0:
```python
import functools
import math

import jax
import jax.numpy as jnp
import numpy as np
from jax import lax
from jax.experimental import pallas as pl
from jax.experimental.pallas import tpu as pltpu
from jax.sharding import PartitionSpec as P

HEADS = 16
KV_HEADS = 4
HEAD = 128
GROUP = HEADS // KV_HEADS
MESH = pl.DeviceIdType.MESH
F32 = jnp.float32
BF16 = jnp.bfloat16


def rope_tables(seq_len):
    half = HEAD // 2
    exponent = -np.arange(half, dtype=np.float32) * np.float32(2.0) / np.float32(HEAD)
    frequency = (np.float64(10000.0) ** exponent.astype(np.float64)).astype(np.float32)
    angles = (np.arange(seq_len, dtype=np.float32)[:, None] * frequency).astype(np.float64)
    cosine, sine = np.cos(angles), np.sin(angles)
    return (
        np.concatenate([cosine, cosine], axis=1).astype(np.float32),
        np.concatenate([-sine, sine], axis=1).astype(np.float32),
    )


def kernel(
    n_dp, n, chunks,
    lengths, list_ids,
    owners_hbm, hidden_hbm, again_hbm, fgain_hbm, cos_hbm, sin_hbm, wq_hbm, wk_hbm, wv_hbm, wo_hbm,
    out_ref,
    hid, normed, again, fgain, cos_t, sin_t, wq, wk, wv, wo,
    owners, acc, last_in, gain2,
    x_send, x_recv, q_send, q_recv, u_send, u_recv, mixed, c_send, c_recv, o_send, o_recv,
    e_send, e_recv,
    load_sem, a2a_send, a2a_recv, round_sem,
    zu_s, zd_s, y_s, x_s, dz_s, dy_s, dx_s, z_r, y_r, x_r, dz_r, dy_r, dx_r,
):
    dp = lax.axis_index("dp")
    f = lax.axis_index("fsdp")
    seq_len, width = hid.shape
    slab = width // n
    depth = n // 2
    total = n_dp * n
    cap = out_ref.shape[2]
    a, b = f // 2, f % 2
    core, x_bit = dp % 2, (dp // 2) % 2
    partner = dp + 1 - 2 * core
    x_peer = dp + 2 - 4 * x_bit

    sources = (wk_hbm, hidden_hbm.at[0], again_hbm, wq_hbm, cos_hbm, sin_hbm, wv_hbm, wo_hbm, fgain_hbm,
               owners_hbm)
    targets = (wk.at[f], hid, again, wq, cos_t, sin_t, wv, wo, fgain, owners)
    loads = [
        pltpu.make_async_copy(s, t, load_sem.at[i])
        for i, (s, t) in enumerate(zip(sources, targets))
    ]
    for load in loads:
        load.start()

    me = dp * n + f

    def wrap(index, size):
        return jnp.where(index >= size, index - size, index)

    def each(low, high, body):
        if high <= 8:
            for t in range(low, high):
                body(t)
        else:
            lax.fori_loop(low, high, lambda t, c: (body(t), c)[1], 0)

    def everyone(body):
        for t in range(n_dp):
            o = wrap(dp + t, n_dp)
            each(1 if t == 0 else 0, n, lambda i: body(o, wrap(f + i, n)))

    barrier = pltpu.get_barrier_semaphore()

    def flip(index, bit):
        return index + bit * (1 - 2 * ((index // bit) % 2))

    peers = [(flip(dp, 1 << i), f) for i in range((n_dp - 1).bit_length())]
    peers += [(dp, flip(f, 1 << i)) for i in range((n - 1).bit_length())]

    def greet(o, g):
        pl.semaphore_signal(barrier, inc=1, device_id=(o, g), device_id_type=MESH)

    for o, g in peers:
        greet(o, g)

    @pl.when(a < depth - 1)
    def _():
        greet(dp, f + 2)

    @pl.when(a > 0)
    def _():
        greet(dp, f - 2)

    inner = jnp.where((a > 0) & (a < depth - 1), 1, 0)
    pl.semaphore_wait(barrier, len(peers) + 1 + inner)

    def greet_all():
        for i, (o, g) in enumerate(peers):
            pl.semaphore_signal(round_sem.at[i], inc=1, device_id=(o, g), device_id_type=MESH)
            pl.semaphore_wait(round_sem.at[i], 1)

    step = slab // chunks

    def piece(pa, pb, offset, rows, send_sem, recv_sem, device):
        part = wk.at[pa * 2 + pb, pl.ds(pl.multiple_of(offset, rows), rows), :]
        return pltpu.make_async_remote_copy(
            src_ref=part, dst_ref=part, send_sem=send_sem, recv_sem=recv_sem,
            device_id=device, device_id_type=MESH,
        )

    def half_at(k, c):
        return k * step + c * (step // 2)

    def quarter_at(k, c, x):
        return half_at(k, c) + x * (step // 4)

    half, quarter = step // 2, step // 4

    def up(pa, k):
        return piece(pa, b, half_at(k, core), half, zu_s.at[pa, k], z_r.at[pa, k], (dp, lax.rem(f + 2, n)))

    def down(pa, k):
        return piece(pa, b, half_at(k, core), half, zd_s.at[pa, k], z_r.at[pa, k], (dp, lax.rem(f + n - 2, n)))

    def cross_y(pa, pb, k):
        return piece(pa, pb, quarter_at(k, core, x_bit), quarter, y_s.at[pa, k], y_r.at[pa, k], (dp, 2 * a + 1 - b))

    def cross_x(pa, k, x):
        return piece(pa, 1 - b, quarter_at(k, core, x), quarter, x_s.at[pa, k], x_r.at[pa, k], (x_peer, f))

    def core_z(pa, k, c):
        return piece(pa, b, half_at(k, c), half, dz_s.at[pa, k], dz_r.at[pa, k], (partner, f))

    def core_y(pa, k, c):
        return piece(pa, 1 - b, quarter_at(k, c, x_bit), quarter, dy_s.at[pa, k], dy_r.at[pa, k], (partner, f))

    def core_x(pa, k, c):
        return piece(pa, 1 - b, quarter_at(k, c, 1 - x_bit), quarter, dx_s.at[pa, k], dx_r.at[pa, k], (partner, f))

    loads[0].wait()
    for k in range(chunks):
        @pl.when(a < depth - 1)
        def _():
            up(a, k).start()

        @pl.when(a > 0)
        def _():
            down(a, k).start()

        cross_y(a, b, k).start()

    def give(slot, send, recv, g):
        pltpu.make_async_remote_copy(
            src_ref=send.at[g], dst_ref=recv.at[f], send_sem=a2a_send.at[slot],
            recv_sem=a2a_recv.at[slot], device_id=(dp, g), device_id_type=MESH,
        ).start()

    def exchange(slot, send, recv):
        each(1, n, lambda t: give(slot, send, recv, wrap(f + t, n)))
        recv[f] = send[f]

    def arrived(slot, recv, count):
        blocks = recv.at[pl.ds(0, count)]
        pltpu.make_async_copy(blocks, blocks, a2a_recv.at[slot]).wait()

    def sent(slot, recv, count):
        blocks = recv.at[pl.ds(0, count)]
        pltpu.make_async_copy(blocks, blocks, a2a_send.at[slot]).wait()

    loads[1].wait()
    loads[2].wait()
    last = lengths[0] - 1
    picks = lax.broadcasted_iota(jnp.int32, (16, seq_len), 1) == last
    picks = jnp.where(picks, 1.0, 0.0).astype(BF16)
    row = jnp.concatenate(
        [
            jnp.dot(picks, hid[:, g * slab:(g + 1) * slab], preferred_element_type=F32)[:1]
            for g in range(n)
        ],
        axis=1,
    )
    scale = lax.rsqrt(jnp.mean(row * row, axis=-1, keepdims=True) + 1e-05)
    row_normed = (row * scale * again[...]).astype(BF16).astype(F32)
    for g in range(n):
        x_send[g] = row_normed[:, g * slab:(g + 1) * slab]
        last_in[g:g + 1, :] = row[:, g * slab:(g + 1) * slab]
    greet_all()
    exchange(0, x_send, x_recv)

    block = 16

    def normalise(i, carry):
        window = pl.ds(pl.multiple_of(i * block, block), block)
        x = hid[window, :].astype(F32)
        r = lax.rsqrt(jnp.mean(x * x, axis=-1, keepdims=True) + 1e-05)
        normed[window, :] = (x * r * again[...]).astype(BF16)
        return carry

    lax.fori_loop(0, seq_len // block, normalise, 0)

    def partial_queries():
        loads[3].wait()
        arrived(0, x_recv, n - 1)
        x_all = jnp.concatenate([x_recv[i] for i in range(n)], axis=0).astype(BF16)
        for h in range(HEADS):
            q_send[:, h, :] = jnp.dot(
                x_all, wq[:, h * HEAD:(h + 1) * HEAD], preferred_element_type=F32
            )
        exchange(1, q_send, q_recv)

    acc[...] = jnp.zeros_like(acc)

    def accumulate(slab_index):
        columns = pl.ds(pl.multiple_of(slab_index * slab, slab), slab)
        acc[...] += jnp.dot(normed[:, columns], wk[slab_index], preferred_element_type=F32)

    accumulate(f)

    def around(e, body):
        for sign in (1, -1):
            pa = a + sign * e
            valid = (pa >= 0) & (pa < depth) & (e >= (0 if sign == 1 else 1))

            @pl.when(valid)
            def _():
                body(pa, sign)

    def gather_step(d, carry):
        def from_z(pa, sign):
            for k in range(chunks):
                up(pa, k).wait_recv()
                if sign == 1:
                    @pl.when(a > 0)
                    def _():
                        down(pa, k).start()
                else:
                    @pl.when(a < depth - 1)
                    def _():
                        up(pa, k).start()
                cross_y(pa, b, k).start()
                core_z(pa, k, core).start()

        def from_y(pa, sign):
            for k in range(chunks):
                cross_y(pa, 1 - b, k).wait_recv()
                cross_x(pa, k, x_bit).start()
                core_y(pa, k, core).start()

        def from_x(pa, sign):
            for k in range(chunks):
                cross_x(pa, k, 1 - x_bit).wait_recv()
                core_x(pa, k, core).start()

        def consume(pa, sign):
            @pl.when(pa != a)
            def _():
                for k in range(chunks):
                    core_z(pa, k, 1 - core).wait_recv()
                accumulate(pa * 2 + b)

            for k in range(chunks):
                core_y(pa, k, 1 - core).wait_recv()
                core_x(pa, k, 1 - core).wait_recv()
            accumulate(pa * 2 + 1 - b)

        @pl.when(d >= 1)
        def _():
            around(d, from_z)
            around(d - 1, from_y)

        @pl.when(d >= 2)
        def _():
            around(d - 2, from_x)

        @pl.when(d == 2)
        def _():
            partial_queries()

        @pl.when(d >= 3)
        def _():
            around(d - 3, consume)

        return carry

    lax.fori_loop(1, depth + 3, gather_step, 0)

    for load in loads[4:]:
        load.wait()
    arrived(1, q_recv, n - 1)
    queries = jnp.sum(q_recv[...], axis=0)
    at_last = lax.broadcasted_iota(jnp.int32, cos_t.shape, 0) == last
    q_cos = jnp.sum(jnp.where(at_last, cos_t[...], 0.0), axis=0, keepdims=True)
    q_sin = jnp.sum(jnp.where(at_last, sin_t[...], 0.0), axis=0, keepdims=True)
    queries = queries * q_cos + pltpu.roll(queries, HEAD // 2, 1) * q_sin
    queries = (queries * (1.0 / math.sqrt(HEAD))).astype(BF16)

    scores = jnp.zeros((HEADS, seq_len), F32)
    head_of = lax.broadcasted_iota(jnp.int32, scores.shape, 0) // GROUP
    for kv in range(KV_HEADS):
        keys = acc[:, kv * HEAD:(kv + 1) * HEAD]
        keys = (keys * cos_t[...] + pltpu.roll(keys, HEAD // 2, 1) * sin_t[...]).astype(BF16)
        part = lax.dot_general(queries, keys, (((1,), (1,)), ((), ())), preferred_element_type=F32)
        scores = jnp.where(head_of == kv, part, scores)
    visible = lax.broadcasted_iota(jnp.int32, scores.shape, 1) < lengths[0]
    scores = jnp.where(visible, scores, -jnp.inf)
    powers = jnp.exp(scores - jnp.max(scores, axis=-1, keepdims=True))
    weights = (powers / jnp.sum(powers, axis=-1, keepdims=True)).astype(BF16)

    def weighted(g):
        columns = pl.ds(pl.multiple_of(g * slab, slab), slab)
        return jnp.dot(weights, normed[:, columns], preferred_element_type=F32)

    for t in range(1, n):
        g = wrap(f + t, n)
        u_send[g] = weighted(g)
        give(2, u_send, u_recv, g)
    u_recv[f] = weighted(f)
    arrived(2, u_recv, n - 1)
    sums = u_recv[...].reshape(n * HEADS, slab)
    top = sums.astype(BF16)
    rest = sums - top.astype(F32)
    middle = rest.astype(BF16)
    low = (rest - middle.astype(F32)).astype(BF16)
    values = wv[...]
    product = (
        jnp.dot(low, values, preferred_element_type=F32)
        + jnp.dot(middle, values, preferred_element_type=F32)
    ) + jnp.dot(top, values, preferred_element_type=F32)
    for kv in range(KV_HEADS):
        mixed[kv] = product[:, kv * HEAD:(kv + 1) * HEAD]

    share = HEADS * HEAD // n
    for h in range(HEADS):
        kv = h // GROUP
        part = mixed[kv, pl.ds(h, n, stride=HEADS), :]
        if share >= HEAD:
            at = h * HEAD % share
            c_send[h * HEAD // share, :, at:at + HEAD] = part
        else:
            pieces = HEAD // share
            for i in range(pieces):
                c_send[h * pieces + i] = part[:, i * share:(i + 1) * share]
    exchange(3, c_send, c_recv)
    arrived(3, c_recv, n - 1)
    context = jnp.sum(c_recv[...], axis=0).astype(BF16)
    for g in range(n):
        o_send[:, g, :] = jnp.dot(
            context, wo[:, g * slab:(g + 1) * slab], preferred_element_type=F32
        )
        gain2[g:g + 1, :] = fgain[:, g * slab:(g + 1) * slab]
    exchange(4, o_send, o_recv)

    lists = lax.broadcasted_iota(jnp.int32, owners.shape, 1)

    def owner_of(r):
        held = jnp.where(lists == list_ids[r], owners[...], 0)
        return jnp.sum(held.astype(F32), axis=1, keepdims=True)

    owner = owner_of(f)

    def count(r, slot):
        same = jnp.where(owner_of(r) == owner, 1.0, 0.0)
        return slot + same * jnp.where(r < f, 1.0, 0.0)

    code = owner * cap + lax.fori_loop(0, n, count, jnp.zeros((1, 1), F32))

    arrived(4, o_recv, n - 1)
    scaled = (last_in[...] + jnp.sum(o_recv[...], axis=0)) * gain2[...]
    square = jnp.sum(jnp.sum(scaled * scaled, axis=1, keepdims=True), axis=0, keepdims=True)
    embedded = (scaled * lax.rsqrt(square / width + 1e-06)).astype(BF16).astype(F32)
    for g in range(n):
        e_send[g, :, :slab] = embedded[g:g + 1, :]
        e_send[g, :, slab:] = jnp.broadcast_to(code, (1, 128))

    def post(o, g):
        pltpu.make_async_remote_copy(
            src_ref=e_send.at[g], dst_ref=e_recv.at[me], send_sem=a2a_send.at[5],
            recv_sem=a2a_recv.at[5], device_id=(o, g), device_id_type=MESH,
        ).start()

    everyone(post)
    e_recv[me] = e_send[f]
    arrived(5, e_recv, total - 1)

    first = (dp * cap).astype(F32)
    for j in range(n_dp):
        rows = jnp.concatenate([e_recv[j * n + i] for i in range(n)], axis=0)
        codes = rows[:, slab:slab + 1]
        for s in range(cap):
            kept = jnp.where(codes == first + s, rows[:, :slab], 0.0)
            out_ref[0, j, s:s + 1, :] = jnp.sum(kept, axis=0, keepdims=True).astype(BF16)

    for index, recv in ((0, x_recv), (1, q_recv), (2, u_recv), (3, c_recv), (4, o_recv)):
        sent(index, recv, n - 1)
    sent(5, e_recv, total - 1)

    def drain(pa, carry):
        for k in range(chunks):
            @pl.when((pa <= a) & (a < depth - 1))
            def _():
                up(pa, k).wait_send()

            @pl.when((pa >= a) & (a > 0))
            def _():
                down(pa, k).wait_send()

            @pl.when(pa != a)
            def _():
                core_z(pa, k, core).wait_send()

            cross_y(pa, b, k).wait_send()
            cross_x(pa, k, x_bit).wait_send()
            core_y(pa, k, core).wait_send()
            core_x(pa, k, core).wait_send()
        return carry

    lax.fori_loop(0, depth, drain, 0)


def local(
    n_dp, n,
    hidden, lengths, list_ids, list_owner, attn_gain, final_gain, w_query, w_key, w_value, w_out,
):
    _, seq_len, width = hidden.shape
    slab = width // n
    depth = n // 2
    chunks = 2 if n <= 8 else 1
    cap = max(2, 2 * n // n_dp)
    share = HEADS * HEAD // n
    cosine, sine = rope_tables(seq_len)
    pieces = pltpu.SemaphoreType.DMA((depth, chunks))
    any_spec = pl.BlockSpec(memory_space=pl.ANY)
    smem_spec = pl.BlockSpec(memory_space=pltpu.SMEM)
    vmem = pltpu.VMEM
    return pl.pallas_call(
        functools.partial(kernel, n_dp, n, chunks),
        out_shape=jax.ShapeDtypeStruct((1, n_dp, cap, slab), BF16),
        in_specs=[smem_spec] * 2 + [any_spec] * 10,
        out_specs=pl.BlockSpec(memory_space=pltpu.VMEM),
        scratch_shapes=[
            vmem((seq_len, width), BF16),
            vmem((seq_len, width), BF16),
            vmem((1, width), F32),
            vmem((1, width), F32),
            vmem((seq_len, HEAD), F32),
            vmem((seq_len, HEAD), F32),
            vmem(w_query.shape, BF16),
            vmem((n,) + w_key.shape, BF16),
            vmem(w_value.shape, BF16),
            vmem(w_out.shape, BF16),
            vmem((1, list_owner.shape[0]), jnp.int32),
            vmem((seq_len, KV_HEADS * HEAD), F32),
            vmem((n, slab), F32),
            vmem((n, slab), F32),
            vmem((n, 1, slab), F32),
            vmem((n, 1, slab), F32),
            vmem((n, HEADS, HEAD), F32),
            vmem((n, HEADS, HEAD), F32),
            vmem((n, HEADS, slab), F32),
            vmem((n, HEADS, slab), F32),
            vmem((KV_HEADS, n * HEADS, HEAD), F32),
            vmem((n, n, share), F32),
            vmem((n, n, share), F32),
            vmem((n, n, slab), F32),
            vmem((n, n, slab), F32),
            vmem((n, 1, slab + 128), F32),
            vmem((n_dp * n, 1, slab + 128), F32),
            pltpu.SemaphoreType.DMA((10,)),
            pltpu.SemaphoreType.DMA((6,)),
            pltpu.SemaphoreType.DMA((6,)),
            pltpu.SemaphoreType.REGULAR(((n_dp - 1).bit_length() + (n - 1).bit_length(),)),
        ] + [pieces] * 13,
        compiler_params=pltpu.CompilerParams(
            collective_id=0, has_side_effects=True, vmem_limit_bytes=67043328
        ),
    )(
        lengths, list_ids,
        list_owner.reshape(1, -1), hidden, attn_gain.reshape(1, width), final_gain.reshape(1, width),
        cosine, sine, w_query, w_key, w_value, w_out,
    )


def solution(mesh):
    in_specs = (
        P(("dp", "fsdp"), None, None),
        P(("dp", "fsdp")),
        P("dp"),
        P(),
        P(),
        P(),
        P("fsdp", None),
        P("fsdp", None),
        P("fsdp", None),
        P("fsdp", None),
    )
    out_specs = P("dp", None, None, "fsdp")
    body = functools.partial(local, mesh.shape["dp"], mesh.shape["fsdp"])
    return jax.shard_map(body, mesh=mesh, in_specs=in_specs, out_specs=out_specs, check_vma=False)
```

profile of v0, /device:TPU:0, one launch (start us, length us, event | category | flops | bytes accessed | tf_op | source)
XLA Modules:
  0.0 62.1 jit_solution(1097957108156620725)
XLA Ops:
  0.7 60.1 %shard_map.118 = bf16[1,4,4,512]{3,2,1,0:T(4,128)(2,1)} custom-call(s32[1]{0:T(128)S(6)} %copy.14.lengths, s32[8]{0:T(128)} %list_ids.1, s32[1,256]{1,0:T(1,128)} %bitcast.5, bf16[1,256,4096]{2,1,0:T(8,128)(2,1)} %hidden_hbm.1, f32[1,4096]{1,0:T(1,128)} %bitcast.3, f32[1,4096]{1,0:T(1,128)} %bitcast.4, f32[256,128]{1,0:T(8,128)} %constant.4.clone.cos_hbm, ...), custom_call_target="tpu_custom_call" | custom-call | tf_op jit(solution)/shard_map/pallas_call | solution.py:447
  60.8 1.3 %copy.15 = bf16[1,4,4,512]{3,2,1,0:T(4,128)(2,1)} copy(bf16[1,4,4,512]{3,2,1,0:T(4,128)(2,1)} %shard_map.118) | data formatting | bytes 32768
where the time goes:
time: 62.4 us; the launch traced here: 62.1 us
  Pallas kernels  60.1 us (96%)
  local copies, waits for them, and re-layouts  1.33 us (2%)
  between operations  0.66 us (1%)
    pallas_call x1, Pallas kernels, local(): pl.pallas_call(functools.partial(kernel, n_dp, n, chunks), out_shape=jax....  60.1 us
    unnamed x1, local copies, waits for them, and re-layouts  1.33 us

commit v1 on v0

v1 whole, which is shorter than its diff:
```python
import functools
import math

import jax
import jax.numpy as jnp
import numpy as np
from jax import lax
from jax.experimental import pallas as pl
from jax.experimental.pallas import tpu as pltpu
from jax.sharding import PartitionSpec as P

HEADS = 16
KV_HEADS = 4
HEAD = 128
GROUP = HEADS // KV_HEADS
CORES = 2
MY_HEADS = HEADS // CORES
MY_KV = KV_HEADS // CORES
UNITS = 8
MESH = pl.DeviceIdType.MESH
F32 = jnp.float32
BF16 = jnp.bfloat16


def rope_tables(seq_len):
    half = HEAD // 2
    exponent = -np.arange(half, dtype=np.float32) * np.float32(2.0) / np.float32(HEAD)
    frequency = (np.float64(10000.0) ** exponent.astype(np.float64)).astype(np.float32)
    angles = (np.arange(seq_len, dtype=np.float32)[:, None] * frequency).astype(np.float64)
    cosine, sine = np.cos(angles), np.sin(angles)
    return (
        np.concatenate([cosine, cosine], axis=1).astype(np.float32),
        np.concatenate([-sine, sine], axis=1).astype(np.float32),
    )


def key_chunks(n):
    if n <= 8:
        return ((0, 1), (1, 2), (2, 3)), ((0, 1), (1, 2))
    return ((0, 3),), ((0, 2),)


def kernel(
    n_dp, n,
    lengths_hbm, ids_hbm,
    owners_hbm, hidden_hbm, again_hbm, fgain_hbm, cos_hbm, sin_hbm, wq_hbm, wk_hbm, wv_hbm, wo_hbm,
    out_ref,
    lengths, list_ids,
    hid, normed, squares, again, fgain, cos_t, sin_t, wq, wk, wv, wo,
    owners, acc, last_in,
    x_send, x_recv, q_send, q_recv, u_send, u_recv, mixed, c_send, c_recv, o_send, o_recv,
    e_send, e_recv, s_send, s_recv,
    load_sem, a2a_send, a2a_recv, norm_send, norm_recv,
    z_s, y_s, x_s, z_r, y_r, x_r,
):
    dp = lax.axis_index("dp")
    f = lax.axis_index("fsdp")
    seq_len, width = hid.shape
    slab = width // n
    depth = n // 2
    total = n_dp * n
    half = n // 2
    cap = out_ref.shape[2]
    a, b = f // 2, f % 2
    core, x_bit = dp % 2, (dp // 2) % 2
    base = dp - core
    partner = base + 1 - core
    x_peer = dp + 2 - 4 * x_bit
    me = dp * n + f
    key_width = wk.shape[2]
    query_width = wq.shape[1]

    def lanes(index, size):
        return pl.ds(pl.multiple_of(index * size, size), size)

    sources = (
        wk_hbm.at[:, lanes(core, key_width)], lengths_hbm, hidden_hbm.at[0], again_hbm,
        wq_hbm.at[:, lanes(core, query_width)], cos_hbm, sin_hbm, wv_hbm.at[:, lanes(core, key_width)], wo_hbm,
        fgain_hbm.at[:, lanes(f, slab)], owners_hbm, ids_hbm,
    )
    targets = (wk.at[f], lengths, hid, again, wq, cos_t, sin_t, wv, wo, fgain, owners, list_ids)
    loads = [
        pltpu.make_async_copy(s, t, load_sem.at[i])
        for i, (s, t) in enumerate(zip(sources, targets))
    ]

    def wrap(index, size):
        return jnp.where(index >= size, index - size, index)

    def each(low, high, body):
        if high <= 8:
            for t in range(low, high):
                body(t)
        else:
            lax.fori_loop(low, high, lambda t, c: (body(t), c)[1], 0)

    def everyone(body):
        for t in range(n_dp):
            o = wrap(dp + t, n_dp)
            each(1 if t == 0 else 0, n, lambda i: body(o, wrap(f + i, n)))

    barrier = pltpu.get_barrier_semaphore()
    everyone(lambda o, g: pl.semaphore_signal(barrier, inc=1, device_id=(o, g), device_id_type=MESH))
    for load in loads:
        load.start()

    unit = slab // UNITS
    alone, shared = key_chunks(n)
    chunks = [(2, 3, lo, hi) for lo, hi in alone] + [(0, 0, lo, hi) for lo, hi in shared]
    n_alone = len(alone)

    def piece(pa, pb, c, column, send_sem, recv_sem, device):
        first, step, lo, hi = chunks[c]
        start = (first + step * column + lo) * unit
        part = wk.at[pa * 2 + pb, pl.ds(pl.multiple_of(start, unit), (hi - lo) * unit), :]
        return pltpu.make_async_remote_copy(
            src_ref=part, dst_ref=part, send_sem=send_sem, recv_sem=recv_sem,
            device_id=device, device_id_type=MESH,
        )

    def far(t):
        return wrap(a + t, depth)

    def along_z(t, c):
        return piece(a, b, c, x_bit, z_s.at[t, c], z_r.at[a, c], (dp, far(t) * 2 + b))

    def from_z(pa, c):
        return piece(pa, b, c, x_bit, z_s.at[0, c], z_r.at[pa, c], (dp, f))

    def along_y(pa, c):
        return piece(pa, b, c, x_bit, y_s.at[pa, c], y_r.at[pa, c], (dp, 2 * a + 1 - b))

    def from_y(pa, c):
        return piece(pa, 1 - b, c, x_bit, y_s.at[pa, c], y_r.at[pa, c], (dp, f))

    def along_x(pa, pb, c):
        return piece(pa, pb, c, x_bit, x_s.at[pa * 2 + pb, c], x_r.at[pa * 2 + pb, c], (x_peer, f))

    def from_x(pa, pb, c):
        return piece(pa, pb, c, 1 - x_bit, x_s.at[pa * 2 + pb, c], x_r.at[pa * 2 + pb, c], (dp, f))

    def others(body):
        each(1, depth, lambda t: body(far(t)))

    def give(slot, src, dst, device):
        pltpu.make_async_remote_copy(
            src_ref=src, dst_ref=dst, send_sem=a2a_send.at[slot],
            recv_sem=a2a_recv.at[slot], device_id=device, device_id_type=MESH,
        ).start()

    def exchange(slot, send, recv):
        each(1, n, lambda t: give(slot, send.at[wrap(f + t, n)], recv.at[f], (dp, wrap(f + t, n))))
        recv[f] = send[f]

    def arrived(slot, recv, count):
        blocks = recv.at[pl.ds(0, count)]
        pltpu.make_async_copy(blocks, blocks, a2a_recv.at[slot]).wait()

    def sent(slot, recv, count):
        blocks = recv.at[pl.ds(0, count)]
        pltpu.make_async_copy(blocks, blocks, a2a_send.at[slot]).wait()

    with jax.named_scope("p_barrier"):
        pl.semaphore_wait(barrier, total - 1)
    with jax.named_scope("p_wkload"):
        loads[0].wait()
    for c in range(len(chunks)):
        along_y(a, c).start()
        each(1, depth, lambda t: along_z(t, c).start())

    with jax.named_scope("p_hidload"):
        for load in loads[1:4]:
            load.wait()
    length = lengths[0]
    picks = lax.broadcasted_iota(jnp.int32, (16, seq_len), 1) == length - 1
    picks = jnp.where(picks, 1.0, 0.0).astype(BF16)
    row = jnp.concatenate(
        [
            jnp.dot(picks, hid[:, g * slab:(g + 1) * slab], preferred_element_type=F32)[:1]
            for g in range(n)
        ],
        axis=1,
    )
    scale = lax.rsqrt(jnp.mean(row * row, axis=-1, keepdims=True) + 1e-05)
    row_normed = (row * scale * again[...]).astype(BF16).astype(F32)
    size = jnp.full((1, 128), length, jnp.int32).astype(F32)
    for g in range(n):
        x_send[g, :, :slab] = row_normed[:, g * slab:(g + 1) * slab]
        x_send[g, :, slab:2 * slab] = row[:, g * slab:(g + 1) * slab]
        x_send[g, :, 2 * slab:] = size
    place = core * n + f
    with jax.named_scope("p_x"):
        each(1, n, lambda t: give(0, x_send.at[wrap(f + t, n)], x_recv.at[place], (dp, wrap(f + t, n))))
        each(0, n, lambda t: give(0, x_send.at[wrap(f + t, n)], x_recv.at[place], (partner, wrap(f + t, n))))
        x_recv[place] = x_send[f]

    block = 16
    blocks = seq_len // block

    def square(i, carry):
        window = pl.ds(pl.multiple_of(i * block, block), block)
        x = hid[window, :].astype(F32)
        x = x * x
        lane_sum = x[:, :128]
        for k in range(1, width // 128):
            lane_sum += x[:, k * 128:(k + 1) * 128]
        squares[window, :] = lane_sum
        return carry

    with jax.named_scope("p_norm"):
        lax.fori_loop(0, blocks, square, 0)
        means = jnp.sum(squares[...], axis=-1, keepdims=True) / width
        squares[...] = jnp.broadcast_to(lax.rsqrt(means + 1e-05), squares.shape)

        def normalise(i, carry):
            window = pl.ds(pl.multiple_of(i * block, block), block)
            into = pl.ds(pl.multiple_of(core * seq_len + i * block, block), block)
            r = squares[window, :1]
            normed[into, :] = (hid[window, :].astype(F32) * r * again[...]).astype(BF16)
            return carry

        quarter = seq_len // 4

        def hand(k):
            part = normed.at[pl.ds(pl.multiple_of(core * seq_len + k * quarter, quarter), quarter), :]
            return pltpu.make_async_remote_copy(
                src_ref=part, dst_ref=part, send_sem=norm_send.at[k], recv_sem=norm_recv.at[k],
                device_id=(partner, f), device_id_type=MESH,
            )

        for k in range(4):
            lax.fori_loop(k * blocks // 4, (k + 1) * blocks // 4, normalise, 0)
            hand(k).start()

    def handed():
        for k in range(4):
            part = normed.at[pl.ds(pl.multiple_of((1 - core) * seq_len + k * quarter, quarter), quarter), :]
            pltpu.make_async_copy(part, part, norm_recv.at[k]).wait()

    def partial_queries():
        loads[4].wait()
        arrived(0, x_recv, 2 * n - 1)
        x_all = jnp.concatenate([x_recv[k, :, :slab] for k in range(2 * n)], axis=0).astype(BF16)
        for h in range(MY_HEADS):
            part = jnp.dot(x_all, wq[:, h * HEAD:(h + 1) * HEAD], preferred_element_type=F32)
            for s in range(CORES):
                q_send[pl.ds(s * MY_HEADS + h, n, stride=CORES * MY_HEADS), :] = part[s * n:(s + 1) * n]
        rows = CORES * MY_HEADS

        def at(g):
            return pl.ds(pl.multiple_of(g * rows, rows), rows)

        each(1, n, lambda t: give(1, q_send.at[at(wrap(f + t, n))], q_recv.at[f], (dp, wrap(f + t, n))))
        q_recv[f] = q_send[at(f), :]

    def codes():
        for load in loads[5:]:
            load.wait()
        for i in range(n):
            last_in[i:i + 1, :] = x_recv[core * n + i][:, slab:2 * slab]
        lists = lax.broadcasted_iota(jnp.int32, (n, owners.shape[1]), 1)
        rows = lax.broadcasted_iota(jnp.int32, (n, owners.shape[1]), 0)
        ids = jnp.zeros((n, owners.shape[1]), jnp.int32)
        for r in range(n):
            ids = jnp.where(rows == r, list_ids[r], ids)
        owner = jnp.sum(jnp.where(lists == ids, owners[...], 0).astype(F32), axis=1, keepdims=True)
        lane = lax.broadcasted_iota(jnp.int32, (n, 128), 1)
        line = lax.broadcasted_iota(jnp.int32, (n, 128), 0)
        owner_row = jnp.sum(jnp.where(lane == line, owner, 0.0), axis=0, keepdims=True)
        earlier = jnp.where((owner_row == owner) & (lane < line), 1.0, 0.0)
        slot = jnp.sum(earlier, axis=1, keepdims=True)
        e_send[:, slab:] = jnp.broadcast_to(owner * cap + slot, (n, 128))

    split = 2 * unit
    parted = split % 128 == 0

    def accumulate(s, low, high):
        columns = pl.ds(pl.multiple_of(s * slab + low, 128), high - low)
        acc[...] += jnp.dot(normed[:, columns], wk[s, low:high, :], preferred_element_type=F32)

    def own_plane(c):
        from_y(a, c).wait_recv()
        if c < n_alone:
            along_x(a, 1 - b, c).start()

    def pass_z(c):
        def body(pa):
            from_z(pa, c).wait_recv()
            along_y(pa, c).start()
            if c < n_alone:
                along_x(pa, b, c).start()
        others(body)

    def pass_y(c):
        def body(pa):
            from_y(pa, c).wait_recv()
            if c < n_alone:
                along_x(pa, 1 - b, c).start()
        others(body)

    with jax.named_scope("g_0"):
        own_plane(0)
        pass_z(0)
    acc[...] = jnp.zeros_like(acc)
    for c in range(1, len(chunks)):
        with jax.named_scope(f"g_z{c}"):
            own_plane(c)
            pass_z(c)
        with jax.named_scope(f"g_y{c}"):
            pass_y(c - 1)
        if c == 1:
            with jax.named_scope("g_q"):
                partial_queries()
                codes()
                handed()
                accumulate(f, 0, slab)

    def first_part(pa, pb):
        for c in range(n_alone):
            from_x(pa, pb, c).wait_recv()
        if parted:
            accumulate(pa * 2 + pb, split, slab)

    with jax.named_scope("g_x"):
        first_part(a, 1 - b)
        others(lambda pa: (first_part(pa, b), first_part(pa, 1 - b)) and None)
    with jax.named_scope("g_last"):
        pass_y(len(chunks) - 1)
    low, high = (0, split) if parted else (0, slab)
    accumulate(a * 2 + 1 - b, low, high)
    others(lambda pa: (accumulate(pa * 2 + b, low, high), accumulate(pa * 2 + 1 - b, low, high)) and None)

    with jax.named_scope("p_qwait"):
        arrived(1, q_recv, n - 1)
    queries = jnp.sum(q_recv[...], axis=0)
    rows = CORES * MY_HEADS
    upper = lax.broadcasted_iota(jnp.int32, (rows, 1), 0) >= MY_HEADS
    size_of = [x_recv[s * n + f][:, 2 * slab:2 * slab + 1] for s in range(CORES)]
    turns = []
    for s in range(CORES):
        token = lax.broadcasted_iota(jnp.int32, cos_t.shape, 0).astype(F32)
        at_last = token == size_of[s] - 1.0
        turns.append([
            jnp.sum(jnp.where(at_last, table[...], 0.0), axis=0, keepdims=True) for table in (cos_t, sin_t)
        ])
    q_cos = jnp.where(upper, turns[1][0], turns[0][0])
    q_sin = jnp.where(upper, turns[1][1], turns[0][1])
    queries = queries * q_cos + pltpu.roll(queries, HEAD // 2, 1) * q_sin
    queries = (queries * (1.0 / math.sqrt(HEAD))).astype(BF16)

    scores = jnp.zeros((rows, seq_len), F32)
    key_of = lax.broadcasted_iota(jnp.int32, scores.shape, 0) // GROUP
    for s in range(CORES):
        for kv in range(MY_KV):
            keys = acc[s * seq_len:(s + 1) * seq_len, kv * HEAD:(kv + 1) * HEAD]
            keys = (keys * cos_t[...] + pltpu.roll(keys, HEAD // 2, 1) * sin_t[...]).astype(BF16)
            part = lax.dot_general(queries, keys, (((1,), (1,)), ((), ())), preferred_element_type=F32)
            scores = jnp.where(key_of == s * MY_KV + kv, part, scores)
    token = lax.broadcasted_iota(jnp.int32, scores.shape, 1).astype(F32)
    visible = token < jnp.where(upper, size_of[1], size_of[0])
    scores = jnp.where(visible, scores, -jnp.inf)
    powers = jnp.exp(scores - jnp.max(scores, axis=-1, keepdims=True))
    weights = powers / jnp.sum(powers, axis=-1, keepdims=True)
    weights = jnp.concatenate(
        [jnp.where(upper, 0.0, weights), jnp.where(upper, weights, 0.0)], axis=1
    ).astype(BF16)

    def weighted(g):
        return jnp.dot(weights, normed[:, lanes(g, slab)], preferred_element_type=F32)

    with jax.named_scope("p_u"):
        for t in range(1, n):
            g = wrap(f + t, n)
            u_send[g] = weighted(g)
            give(2, u_send.at[g], u_recv.at[f], (dp, g))
        u_recv[f] = weighted(f)
    with jax.named_scope("p_uwait"):
        arrived(2, u_recv, n - 1)
    sums = u_recv[...].reshape(n * rows, slab)
    top = sums.astype(BF16)
    rest = sums - top.astype(F32)
    middle = rest.astype(BF16)
    low_part = (rest - middle.astype(F32)).astype(BF16)
    values = wv[...]
    product = (
        jnp.dot(low_part, values, preferred_element_type=F32)
        + jnp.dot(middle, values, preferred_element_type=F32)
    ) + jnp.dot(top, values, preferred_element_type=F32)
    for kv in range(MY_KV):
        mixed[kv] = product[:, kv * HEAD:(kv + 1) * HEAD]

    share = HEADS * HEAD // n
    for s in range(CORES):
        for h in range(MY_HEADS):
            part = mixed[h // GROUP, pl.ds(s * MY_HEADS + h, n, stride=rows), :]
            if share >= HEAD:
                at = h * HEAD % share
                c_send[s * half + h * HEAD // share, :, at:at + HEAD] = part
            else:
                pieces = HEAD // share
                for i in range(pieces):
                    c_send[s * half + h * pieces + i] = part[:, i * share:(i + 1) * share]

    mine = f // half == core
    other_core = 1 - core

    def context_to(s, t):
        k = lax.rem(f + t, half)
        give(3, c_send.at[s * half + k], c_recv.at[f], (base + s, core * half + k))

    each(1, half, lambda t: context_to(core, t))
    each(0, half, lambda t: context_to(other_core, t))

    @pl.when(mine)
    def _():
        c_recv[f] = c_send[core * half + lax.rem(f, half)]
        arrived(3, c_recv, n - 1)

    @pl.when(jnp.logical_not(mine))
    def _():
        context_to(core, 0)
        arrived(3, c_recv, n)

    context = jnp.sum(c_recv[...], axis=0).astype(BF16)

    def projected(g):
        return jnp.dot(context, wo[:, lanes(g, slab)], preferred_element_type=F32)

    with jax.named_scope("p_o"):
        for t in range(1, n):
            g = wrap(f + t, n)
            o_send[g] = projected(g)
            give(4, o_send.at[g], o_recv.at[f], (dp, g))
        o_recv[f] = projected(f)
    with jax.named_scope("p_owait"):
        arrived(4, o_recv, n - 1)
    scaled = (last_in[...] + jnp.sum(o_recv[...], axis=0)) * fgain[...]
    lane = lax.broadcasted_iota(jnp.int32, (n, 128), 1)
    line = lax.broadcasted_iota(jnp.int32, (n, 128), 0)
    summed = jnp.sum(scaled * scaled, axis=1, keepdims=True)
    s_send[...] = jnp.sum(jnp.where(lane == line, summed, 0.0), axis=0, keepdims=True)
    everyone(lambda o, g: give(6, s_send, s_recv.at[me], (o, g)))
    e_send[:, :slab] = scaled
    for t in range(1, n_dp):
        give(5, e_send, e_recv.at[dp], (wrap(dp + t, n_dp), f))
    s_recv[me] = s_send[...]
    e_recv[dp] = e_send[...]
    with jax.named_scope("p_ewait"):
        arrived(5, e_recv, n_dp - 1)
        arrived(6, s_recv, total - 1)

    first = (dp * cap).astype(F32)
    for j in range(n_dp):
        sum_row = jnp.sum(s_recv[j * n:(j + 1) * n], axis=0)
        squared = jnp.sum(jnp.where(lane == line, sum_row, 0.0), axis=1, keepdims=True)
        embedded = e_recv[j, :, :slab] * lax.rsqrt(squared / width + 1e-06)
        embedded = embedded.astype(BF16).astype(F32)
        owner_slot = e_recv[j, :, slab:slab + 1]
        for s in range(cap):
            kept = jnp.where(owner_slot == first + s, embedded, 0.0)
            out_ref[0, j, s:s + 1, :] = jnp.sum(kept, axis=0, keepdims=True).astype(BF16)

    with jax.named_scope("p_sent"):
        sent(0, x_recv, 2 * n - 1)
        for slot, recv in ((1, q_recv), (2, u_recv), (4, o_recv)):
            sent(slot, recv, n - 1)

        @pl.when(mine)
        def _():
            sent(3, c_recv, n - 1)

        @pl.when(jnp.logical_not(mine))
        def _():
            sent(3, c_recv, n)

        sent(5, e_recv, n_dp - 1)
        sent(6, s_recv, total - 1)
        for k in range(4):
            hand(k).wait_send()
    with jax.named_scope("p_drain"):
        for c in range(len(chunks)):
            each(1, depth, lambda t: along_z(t, c).wait_send())
            each(0, depth, lambda t: along_y(far(t), c).wait_send())
            if c < n_alone:
                along_x(a, 1 - b, c).wait_send()
                others(lambda pa: (along_x(pa, b, c).wait_send(), along_x(pa, 1 - b, c).wait_send()) and None)


def local(
    n_dp, n,
    hidden, lengths, list_ids, list_owner, attn_gain, final_gain, w_query, w_key, w_value, w_out,
):
    _, seq_len, width = hidden.shape
    slab = width // n
    depth = n // 2
    cap = max(2, 2 * n // n_dp)
    share = HEADS * HEAD // n
    cosine, sine = rope_tables(seq_len)
    alone, shared = key_chunks(n)
    dma = pltpu.SemaphoreType.DMA
    any_spec = pl.BlockSpec(memory_space=pl.ANY)
    vmem = pltpu.VMEM
    key_width = w_key.shape[1] // CORES
    rows = CORES * MY_HEADS
    return pl.pallas_call(
        functools.partial(kernel, n_dp, n),
        out_shape=jax.ShapeDtypeStruct((1, n_dp, cap, slab), BF16),
        in_specs=[any_spec] * 12,
        out_specs=pl.BlockSpec(memory_space=pltpu.VMEM),
        scratch_shapes=[
            pltpu.SMEM(lengths.shape, jnp.int32),
            pltpu.SMEM(list_ids.shape, jnp.int32),
            vmem((seq_len, width), BF16),
            vmem((CORES * seq_len, width), BF16),
            vmem((seq_len, 128), F32),
            vmem((1, width), F32),
            vmem((1, slab), F32),
            vmem((seq_len, HEAD), F32),
            vmem((seq_len, HEAD), F32),
            vmem((w_query.shape[0], w_query.shape[1] // CORES), BF16),
            vmem((n, slab, key_width), BF16),
            vmem((slab, key_width), BF16),
            vmem(w_out.shape, BF16),
            vmem((1, list_owner.shape[0]), jnp.int32),
            vmem((CORES * seq_len, key_width), F32),
            vmem((n, slab), F32),
            vmem((n, 1, 2 * slab + 128), F32),
            vmem((CORES * n, 1, 2 * slab + 128), F32),
            vmem((n * rows, HEAD), F32),
            vmem((n, rows, HEAD), F32),
            vmem((n, rows, slab), F32),
            vmem((n, rows, slab), F32),
            vmem((MY_KV, n * rows, HEAD), F32),
            vmem((n, n, share), F32),
            vmem((n, n, share), F32),
            vmem((n, n, slab), F32),
            vmem((n, n, slab), F32),
            vmem((n, slab + 128), F32),
            vmem((n_dp, n, slab + 128), F32),
            vmem((1, 128), F32),
            vmem((n_dp * n, 1, 128), F32),
            dma((12,)),
            dma((7,)),
            dma((7,)),
            dma((4,)),
            dma((4,)),
            dma((depth, len(alone) + len(shared))),
            dma((depth, len(alone) + len(shared))),
            dma((n, len(alone))),
            dma((depth, len(alone) + len(shared))),
            dma((depth, len(alone) + len(shared))),
            dma((n, len(alone))),
        ],
        compiler_params=pltpu.CompilerParams(
            collective_id=0, has_side_effects=True, vmem_limit_bytes=67043328
        ),
    )(
        lengths, list_ids,
        list_owner.reshape(1, -1), hidden, attn_gain.reshape(1, width), final_gain.reshape(1, width),
        cosine, sine, w_query, w_key, w_value, w_out,
    )


def solution(mesh):
    in_specs = (
        P(("dp", "fsdp"), None, None),
        P(("dp", "fsdp")),
        P("dp"),
        P(),
        P(),
        P(),
        P("fsdp", None),
        P("fsdp", None),
        P("fsdp", None),
        P("fsdp", None),
    )
    out_specs = P("dp", None, None, "fsdp")
    body = functools.partial(local, mesh.shape["dp"], mesh.shape["fsdp"])
    return jax.shard_map(body, mesh=mesh, in_specs=in_specs, out_specs=out_specs, check_vma=False)
```

time: 62.4 us -> 63.2 us (1.013)
  Pallas kernels: 60.1 us -> 61 us
    pallas_call x1, Pallas kernels: 60.1 us -> 61 us  [local(): pl.pallas_call(functools.partial(kernel, n_dp, n), out_shape=jax.ShapeDty...]
where the time goes in v1:
time: 63.2 us; the launch traced here: 63 us
  Pallas kernels  61 us (97%)
  local copies, waits for them, and re-layouts  1.33 us (2%)
  between operations  0.66 us (1%)
    pallas_call x1, Pallas kernels, local(): pl.pallas_call(functools.partial(kernel, n_dp, n), out_shape=jax.ShapeDty...  61 us
    unnamed x1, local copies, waits for them, and re-layouts  1.33 us

profile of v1, /device:TPU:0, one launch (start us, length us, event | category | flops | bytes accessed | tf_op | source)
XLA Modules:
  0.0 63.0 jit_solution(7758196735805056518)
XLA Ops:
  0.7 61.0 %shard_map.118 = bf16[1,4,4,512]{3,2,1,0:T(4,128)(2,1)} custom-call(s32[1]{0:T(128)S(6)} %copy.14.lengths_hbm, s32[8]{0:T(128)} %ids_hbm.1, s32[1,256]{1,0:T(1,128)} %bitcast.5, bf16[1,256,4096]{2,1,0:T(8,128)(2,1)} %hidden_hbm.1, f32[1,4096]{1,0:T(1,128)} %bitcast.3, f32[1,4096]{1,0:T(1,128)} %bitcast.4, f32[256,128]{1,0:T(8,128)} %constant.4.clone.cos_hbm, ...), custom_call_target="tpu_custom_call" | custom-call | tf_op jit(solution)/shard_map/pallas_call | solution.py:505
  61.6 1.3 %copy.15 = bf16[1,4,4,512]{3,2,1,0:T(4,128)(2,1)} copy(bf16[1,4,4,512]{3,2,1,0:T(4,128)(2,1)} %shard_map.118) | data formatting | bytes 32768

commit v2 on v1

--- a/solution.py
+++ b/solution.py
@@ -164,10 +164,12 @@
         pl.semaphore_wait(barrier, total - 1)
     with jax.named_scope("p_wkload"):
         loads[0].wait()
-    for c in range(len(chunks)):
+
+    def spread(c):
         along_y(a, c).start()
         each(1, depth, lambda t: along_z(t, c).start())
 
+    spread(0)
     with jax.named_scope("p_hidload"):
         for load in loads[1:4]:
             load.wait()
@@ -191,10 +193,11 @@
     place = core * n + f
     with jax.named_scope("p_x"):
         each(1, n, lambda t: give(0, x_send.at[wrap(f + t, n)], x_recv.at[place], (dp, wrap(f + t, n))))
-        each(0, n, lambda t: give(0, x_send.at[wrap(f + t, n)], x_recv.at[place], (partner, wrap(f + t, n))))
+        for c in range(1, len(chunks)):
+            spread(c)
         x_recv[place] = x_send[f]
 
-    block = 16
+    block = 32
     blocks = seq_len // block
 
     def square(i, carry):
@@ -237,9 +240,17 @@
             part = normed.at[pl.ds(pl.multiple_of((1 - core) * seq_len + k * quarter, quarter), quarter), :]
             pltpu.make_async_copy(part, part, norm_recv.at[k]).wait()
 
+    def hand_rows():
+        part = x_recv.at[pl.ds(pl.multiple_of(core * n, n), n)]
+        return pltpu.make_async_remote_copy(
+            src_ref=part, dst_ref=part, send_sem=norm_send.at[4], recv_sem=norm_recv.at[4],
+            device_id=(partner, f), device_id_type=MESH,
+        )
+
     def partial_queries():
         loads[4].wait()
-        arrived(0, x_recv, 2 * n - 1)
+        part = x_recv.at[pl.ds(pl.multiple_of((1 - core) * n, n), n)]
+        pltpu.make_async_copy(part, part, norm_recv.at[4]).wait()
         x_all = jnp.concatenate([x_recv[k, :, :slab] for k in range(2 * n)], axis=0).astype(BF16)
         for h in range(MY_HEADS):
             part = jnp.dot(x_all, wq[:, h * HEAD:(h + 1) * HEAD], preferred_element_type=F32)
@@ -278,6 +289,8 @@
         columns = pl.ds(pl.multiple_of(s * slab + low, 128), high - low)
         acc[...] += jnp.dot(normed[:, columns], wk[s, low:high, :], preferred_element_type=F32)
 
+    assert len(shared) >= 2 or n > 8
+
     def own_plane(c):
         from_y(a, c).wait_recv()
         if c < n_alone:
@@ -298,37 +311,57 @@
                 along_x(pa, 1 - b, c).start()
         others(body)
 
+    last_chunk = len(chunks) - 1
+    low, high = (0, split) if parted else (0, slab)
+
+    def first_part(s, ready):
+        for c in range(n_alone):
+            ready(c)
+        if parted:
+            accumulate(s, split, slab)
+
     with jax.named_scope("g_0"):
         own_plane(0)
         pass_z(0)
+    with jax.named_scope("g_rows"):
+        arrived(0, x_recv, n - 1)
+        hand_rows().start()
     acc[...] = jnp.zeros_like(acc)
     for c in range(1, len(chunks)):
         with jax.named_scope(f"g_z{c}"):
             own_plane(c)
             pass_z(c)
         with jax.named_scope(f"g_y{c}"):
-            pass_y(c - 1)
+            if c < last_chunk:
+                pass_y(c - 1)
         if c == 1:
             with jax.named_scope("g_q"):
                 partial_queries()
                 codes()
+        if c == min(2, last_chunk):
+            with jax.named_scope("g_own"):
                 handed()
                 accumulate(f, 0, slab)
-
-    def first_part(pa, pb):
+    with jax.named_scope("g_plane"):
         for c in range(n_alone):
-            from_x(pa, pb, c).wait_recv()
+            from_x(a, 1 - b, c).wait_recv()
+        accumulate(a * 2 + 1 - b, 0, slab)
+    with jax.named_scope("g_x"):
+        others(lambda pa: first_part(pa * 2 + b, lambda c: from_x(pa, b, c).wait_recv()))
+    with jax.named_scope("g_last"):
+        pass_y(last_chunk - 1)
+        pass_y(last_chunk)
+    with jax.named_scope("g_xy"):
+        others(lambda pa: first_part(pa * 2 + 1 - b, lambda c: from_x(pa, 1 - b, c).wait_recv()))
+    with jax.named_scope("g_end"):
         if parted:
-            accumulate(pa * 2 + pb, split, slab)
-
-    with jax.named_scope("g_x"):
-        first_part(a, 1 - b)
-        others(lambda pa: (first_part(pa, b), first_part(pa, 1 - b)) and None)
-    with jax.named_scope("g_last"):
-        pass_y(len(chunks) - 1)
-    low, high = (0, split) if parted else (0, slab)
-    accumulate(a * 2 + 1 - b, low, high)
-    others(lambda pa: (accumulate(pa * 2 + b, low, high), accumulate(pa * 2 + 1 - b, low, high)) and None)
+            for t in range(1, depth):
+                shards = [far(t) * 2 + pb for pb in range(2)]
+                left = jnp.concatenate([normed[:, pl.ds(pl.multiple_of(s * slab, 128), split)] for s in shards], axis=1)
+                right = jnp.concatenate([wk[s, :split, :] for s in shards], axis=0)
+                acc[...] += jnp.dot(left, right, preferred_element_type=F32)
+        else:
+            others(lambda pa: (accumulate(pa * 2 + b, low, high), accumulate(pa * 2 + 1 - b, low, high)) and None)
 
     with jax.named_scope("p_qwait"):
         arrived(1, q_recv, n - 1)
@@ -365,27 +398,21 @@
         [jnp.where(upper, 0.0, weights), jnp.where(upper, weights, 0.0)], axis=1
     ).astype(BF16)
 
+    spread_order = sorted(range(1, n), key=lambda t: (abs(t - half), t))
+
     def weighted(g):
         return jnp.dot(weights, normed[:, lanes(g, slab)], preferred_element_type=F32)
 
     with jax.named_scope("p_u"):
-        for t in range(1, n):
+        for t in spread_order:
             g = wrap(f + t, n)
-            u_send[g] = weighted(g)
+            u_send[g] = weighted(g).astype(BF16)
             give(2, u_send.at[g], u_recv.at[f], (dp, g))
-        u_recv[f] = weighted(f)
+        u_recv[f] = weighted(f).astype(BF16)
     with jax.named_scope("p_uwait"):
         arrived(2, u_recv, n - 1)
     sums = u_recv[...].reshape(n * rows, slab)
-    top = sums.astype(BF16)
-    rest = sums - top.astype(F32)
-    middle = rest.astype(BF16)
-    low_part = (rest - middle.astype(F32)).astype(BF16)
-    values = wv[...]
-    product = (
-        jnp.dot(low_part, values, preferred_element_type=F32)
-        + jnp.dot(middle, values, preferred_element_type=F32)
-    ) + jnp.dot(top, values, preferred_element_type=F32)
+    product = jnp.dot(sums, wv[...], preferred_element_type=F32)
     for kv in range(MY_KV):
         mixed[kv] = product[:, kv * HEAD:(kv + 1) * HEAD]
 
@@ -427,14 +454,14 @@
         return jnp.dot(context, wo[:, lanes(g, slab)], preferred_element_type=F32)
 
     with jax.named_scope("p_o"):
-        for t in range(1, n):
+        for t in spread_order:
             g = wrap(f + t, n)
-            o_send[g] = projected(g)
+            o_send[g] = projected(g).astype(BF16)
             give(4, o_send.at[g], o_recv.at[f], (dp, g))
-        o_recv[f] = projected(f)
+        o_recv[f] = projected(f).astype(BF16)
     with jax.named_scope("p_owait"):
         arrived(4, o_recv, n - 1)
-    scaled = (last_in[...] + jnp.sum(o_recv[...], axis=0)) * fgain[...]
+    scaled = (last_in[...] + jnp.sum(o_recv[...].astype(F32), axis=0)) * fgain[...]
     lane = lax.broadcasted_iota(jnp.int32, (n, 128), 1)
     line = lax.broadcasted_iota(jnp.int32, (n, 128), 0)
     summed = jnp.sum(scaled * scaled, axis=1, keepdims=True)
@@ -461,8 +488,8 @@
             out_ref[0, j, s:s + 1, :] = jnp.sum(kept, axis=0, keepdims=True).astype(BF16)
 
     with jax.named_scope("p_sent"):
-        sent(0, x_recv, 2 * n - 1)
-        for slot, recv in ((1, q_recv), (2, u_recv), (4, o_recv)):
+        hand_rows().wait_send()
+        for slot, recv in ((0, x_recv), (1, q_recv), (2, u_recv), (4, o_recv)):
             sent(slot, recv, n - 1)
 
         @pl.when(mine)
@@ -528,13 +555,13 @@
             vmem((CORES * n, 1, 2 * slab + 128), F32),
             vmem((n * rows, HEAD), F32),
             vmem((n, rows, HEAD), F32),
-            vmem((n, rows, slab), F32),
-            vmem((n, rows, slab), F32),
+            vmem((n, rows, slab), BF16),
+            vmem((n, rows, slab), BF16),
             vmem((MY_KV, n * rows, HEAD), F32),
             vmem((n, n, share), F32),
             vmem((n, n, share), F32),
-            vmem((n, n, slab), F32),
-            vmem((n, n, slab), F32),
+            vmem((n, n, slab), BF16),
+            vmem((n, n, slab), BF16),
             vmem((n, slab + 128), F32),
             vmem((n_dp, n, slab + 128), F32),
             vmem((1, 128), F32),
@@ -542,8 +569,8 @@
             dma((12,)),
             dma((7,)),
             dma((7,)),
-            dma((4,)),
-            dma((4,)),
+            dma((5,)),
+            dma((5,)),
             dma((depth, len(alone) + len(shared))),
             dma((depth, len(alone) + len(shared))),
             dma((n, len(alone))),

time: 63.2 us -> 56.2 us (0.89)
  Pallas kernels: 61 us -> 54 us
    pallas_call x1, Pallas kernels: 61 us -> 54 us  [local(): pl.pallas_call(functools.partial(kernel, n_dp, n), out_shape=jax.ShapeDty...]
where the time goes in v2:
time: 56.2 us; the launch traced here: 56 us
  Pallas kernels  54 us (96%)
  local copies, waits for them, and re-layouts  1.33 us (2%)
  between operations  0.66 us (1%)
    pallas_call x1, Pallas kernels, local(): pl.pallas_call(functools.partial(kernel, n_dp, n), out_shape=jax.ShapeDty...  54 us
    unnamed x1, local copies, waits for them, and re-layouts  1.33 us

profile of v2, /device:TPU:0, one launch (start us, length us, event | category | flops | bytes accessed | tf_op | source)
XLA Modules:
  0.0 56.0 jit_solution(12835890632953246423)
XLA Ops:
  0.7 54.0 %shard_map.118 = bf16[1,4,4,512]{3,2,1,0:T(4,128)(2,1)} custom-call(s32[1]{0:T(128)S(6)} %copy.14.lengths_hbm, s32[8]{0:T(128)} %ids_hbm.1, s32[1,256]{1,0:T(1,128)} %bitcast.5, bf16[1,256,4096]{2,1,0:T(8,128)(2,1)} %hidden_hbm.1, f32[1,4096]{1,0:T(1,128)} %bitcast.3, f32[1,4096]{1,0:T(1,128)} %bitcast.4, f32[256,128]{1,0:T(8,128)} %constant.4.clone.cos_hbm, ...), custom_call_target="tpu_custom_call" | custom-call | tf_op jit(solution)/shard_map/pallas_call | solution.py:532
  54.6 1.3 %copy.15 = bf16[1,4,4,512]{3,2,1,0:T(4,128)(2,1)} copy(bf16[1,4,4,512]{3,2,1,0:T(4,128)(2,1)} %shard_map.118) | data formatting | bytes 32768
